TPU v7x, 128 devices: a whole 4x4x4 slice. The times are simulated.
128 devices in a mesh: wide: 32 (over z, y, x_hi), narrow: 4 (over x_lo, core).
Axes of the slice: x: 4 (x_hi: 2, x_lo: 2; x = x_hi * 2 + x_lo), y: 4, z: 4, core: 2. Of those that a mesh axis runs over, the one named last changes fastest.
Arguments:
- image_tower: bfloat16 [64, 2560, 1024], P('wide', 'narrow'), may hold values from -150 to 150
- text_tower: bfloat16 [163840, 1024], P(('wide', 'narrow')), may hold values from -150 to 150
- image_proj: bfloat16 [2, 1024, 768], replicated, may hold values from -1 to 1
- text_proj: bfloat16 [2, 1024, 768], replicated, may hold values from -1 to 1
- logit_scale: float32 [2], replicated, may hold values from 8 to 300
- pair_ids: int32 [163840], P(('wide', 'narrow')), may hold values from 0 to 163839, each once
- band_index: int32 [1], replicated, may hold values from 0 to 63
Outputs:
- learnability: float32 [2560], P('narrow')
- column_lse: float32 [2, 163840], P(None, ('wide', 'narrow'))
Inputs may be any that keep to these rules, and one draw needn't show every extreme that they name: Text t is paired with image pair_ids[t], numbered band * 2560 + position in the band; every image has exactly one text.
All inputs are finite; a program needn't handle non-finite values.
Results may differ from a plain program's by a relative error of at most 0.0041.
Values may be sent and summed in bfloat16 or wider, within the bound.
No kernel may reach another device: no remote copies, remote signals or barrier semaphores. Data moves between devices by JAX's collectives and lax.ppermute only.
A program may use at most 128 MiB of HBM per device.

v0:
```python
import jax
import jax.numpy as jnp
from jax import lax
from jax.sharding import Mesh
from jax.sharding import PartitionSpec as P

WIDE = ("wide_0", "wide_1", "wide_2")
NARROW = ("narrow_0", "narrow_1")
WIDE_NARROW = ("wide_0", "wide_1", "wide_2", "narrow_0", "narrow_1")


def filled_up(lines, size):
    spare = -lines.shape[0] % size
    if not spare:
        return lines
    return jnp.concatenate([lines, jnp.zeros((spare, *lines.shape[1:]), lines.dtype)])


def from_root(value, axis, root):
    lines = jnp.where(lax.axis_index(axis) == root, value, jnp.zeros_like(value)).reshape(
        -1, *value.shape[1:][-1:]
    )
    padded = filled_up(lines, lax.axis_size(axis))
    own = lax.psum_scatter(padded, axis, scatter_dimension=0, tiled=True)
    return lax.all_gather(own, axis, axis=0, tiled=True)[: len(lines)].reshape(value.shape)


def collected_together(value, axis):
    leaves = jax.tree.leaves(value)
    order = sorted(range(len(leaves)), key=lambda k: -leaves[k].size)
    width = (1, *leaves[order[0]].shape)[-1]
    lines = [
        jnp.pad(leaves[k].reshape(-1), (0, -leaves[k].size % width)).reshape(-1, width)
        for k in order
    ]
    both, at, found = (lax.all_gather(jnp.concatenate(lines), axis), 0, {})
    for k, line in zip(order, lines):
        share = both[:, at : at + len(line)].reshape(len(both), -1)
        found[k] = share[:, : leaves[k].size].reshape(-1, *leaves[k].shape)
        at += len(line)
    numbers = iter(range(len(leaves)))
    return jax.tree.map(lambda _: found[next(numbers)], value)


def joined_all(value, axes, combine):
    for axis in axes:
        pieces = collected_together(value, axis)
        value = jax.tree.map(lambda part: part[0], pieces)
        for k in range(1, lax.axis_size(axis)):
            value = combine(value, jax.tree.map(lambda part: part[k], pieces))
    return value


def embed(tower, weight):
    full = jnp.dot(tower, weight, preferred_element_type=jnp.float32)
    return (full * lax.rsqrt(jnp.sum(full * full, axis=-1, keepdims=True) + 1e-06)).astype(
        jnp.bfloat16
    )


def both_heads(tower, weights):
    return jnp.stack([embed(tower, weights[0]), embed(tower, weights[1])])


def join_rows(first, second):
    top = jnp.maximum(first[0], second[0])
    total = first[1] * jnp.exp(first[0] - top) + second[1] * jnp.exp(second[0] - top)
    return (top, total, first[2] + second[2])


def per_device(image_tower, text_tower, image_proj, text_proj, logit_scale, pair_ids, band_index):
    held = image_tower.shape[0]
    rows = image_tower.shape[1]
    text_count = text_tower.shape[0]
    picked = band_index[0]
    owner = picked // held
    mine = lax.dynamic_index_in_dim(image_tower, picked % held, 0, keepdims=False)
    band_rows = from_root(mine, WIDE, owner)
    band_emb = both_heads(band_rows, image_proj)
    text_emb = both_heads(text_tower, text_proj)
    scale = logit_scale[:, None, None]
    position = lax.axis_index(NARROW)
    groups = lax.axis_size(NARROW)
    band_size = rows * groups
    start_max = jnp.full((2, text_count), -1e30, jnp.float32)
    piece = lax.all_gather(band_emb, NARROW, axis=1, tiled=True)
    col_max = start_max
    count = piece.shape[1]
    logits = scale * jnp.einsum("hid,hjd->hij", piece, text_emb, preferred_element_type=jnp.float32)
    target = picked * band_size + jnp.arange(count, dtype=jnp.int32)
    top = jnp.max(logits, axis=2)
    total = jnp.sum(jnp.exp(logits - top[:, :, None]), axis=2)
    hits = pair_ids[None, :] == target[:, None]
    found = jnp.sum(jnp.where(hits[None], logits, 0.0), axis=2)
    row_max = top
    row_sum = total
    row_pos = found
    new_max = jnp.maximum(col_max, jnp.max(logits, axis=1))
    col_sum = jnp.sum(jnp.exp(logits - new_max[:, None, :]), axis=1)
    row_max, row_sum, row_pos, col_max, col_sum = (row_max, row_sum, row_pos, new_max, col_sum)
    column_lse = col_max + jnp.log(col_sum)
    row_max, row_sum, row_pos = joined_all((row_max, row_sum, row_pos), WIDE_NARROW, join_rows)
    losses = row_max + jnp.log(row_sum) - row_pos
    learnability = lax.dynamic_slice_in_dim(losses[0] - losses[1], position * rows, rows, 0)
    return (learnability, column_lse)


def solution(mesh):
    split = Mesh(
        mesh.devices.reshape(4, 4, 2, 2, 2), ("wide_0", "wide_1", "wide_2", "narrow_0", "narrow_1")
    )
    placed = (P(WIDE, NARROW, None), P(WIDE_NARROW, None), P(), P(), P(), P(WIDE_NARROW), P())
    return jax.shard_map(
        per_device,
        mesh=split,
        in_specs=placed,
        out_specs=(P(NARROW), P(None, WIDE_NARROW)),
        check_vma=False,
    )
```

profile of v0, /device:TPU:1, one launch (start us, length us, event | category | flops | bytes accessed | tf_op | source)
XLA Modules:
  0.0 385.2 jit_solution(3234254604567877896)
XLA Ops:
  8.1 2.5 select_bitcast_fusion
  10.6 99.7 %fusion = bf16[24,1024]{1,0:T(8,128)(2,1)S(1)} fusion(bf16[640,1024]{1,0:T(8,128)(2,1)} %select_bitcast_fusion), kind=kCustom, calls=%all-reduce-scatter | all-reduce-scatter fusion | flops 786433 | bytes 1360384
  110.2 1.3 collective-permute-start.5
  111.5 1.3 collective-permute-start
  112.8 1.3 collective-permute-start.1
  114.1 1.3 collective-permute-start.2
  115.4 2.9 collective-permute-start.3
  118.4 1.4 collective-permute-start.4
  119.8 0.6 dynamic-slice.5
  121.1 1.0 concatenate.20
  122.1 0.6 dynamic-slice_bitcast_fusion
  122.8 93.5 %all-gather.16.cloned.1.call-done = bf16[32,20,1024]{2,1,0:T(8,128)(2,1)} async-done(((bf16[1,20,1024]{2,1,0:T(8,128)(2,1)}), bf16[32,20,1024]{2,1,0:T(8,128)(2,1)}) %all-gather.16.cloned.1.call-update) | async-done | bytes 1310736 | tf_op jit(solution)/shard_map/all_gather | solution.py:25
  216.3 3.3 reshape.115
  219.6 3.2 multiply_reduce_fusion.2
  222.9 1.3 multiply_reduce_fusion.3
  224.2 0.3 fusion.18
  224.5 1.4 pad_maximum_fusion
  226.0 4.0 %multiply_reduce_fusion = (f32[1280]{0:T(1024)S(1)}, f32[1280,768]{0,1:T(8,128)S(1)}) fusion(bf16[1280,1024]{1,0:T(8,128)(2,1)S(1)} %copy-done, bf16[2,1024,768]{2,1,0:T(8,128)(2,1)} %param.10), kind=kOutput, calls=%fused_computation.9 | convolution fusion | flops 2015230720 | bytes 8131584 | tf_op jit(solution)/shard_map/dot_general | solution.py:55
  230.0 2.4 multiply_reduce_fusion.1
  232.4 2.0 fusion.4
  234.4 3.6 broadcast_compare_fusion
  238.0 65.2 %all-gather.14.cloned.1.call-done = bf16[2,2560,768]{2,1,0:T(8,128)(2,1)} async-done(((bf16[2,640,768]{2,1,0:T(8,128)(2,1)}), bf16[2,2560,768]{2,1,0:T(8,128)(2,1)}) %all-gather.14.cloned.1.call-update) | async-done | bytes 7864336 | tf_op jit(solution)/shard_map/all_gather | solution.py:86
  303.3 19.6 %fusion.66 = (f32[2,1280]{1,0:T(2,128)S(1)}, f32[2,2560]{1,0:T(2,128)S(1)}, f32[2,2560,1280]{1,2,0:T(8,128)}) fusion(bf16[2,2560,768]{2,1,0:T(8,128)(2,1)} %all-gather.14.cloned.1.call-done, bf16[1,1280,768]{1,2,0:T(8,128)(2,1)} %get-tuple-element.29, bf16[1,1280,768]{1,2,0:T(8,128)(2,1)S(1)} %get-tuple-element.28, f32[2]{0:T(128)S(1)} %copy-done.7), kind=kOutput, calls=%fused_computation.132 | convolution fusion | flops 10087949312 | bytes 38041608 | tf_op jit(solution)/shard_map/hid,hjd->hij/dot_general | solution.py:89
  322.9 15.4 %exponential_reduce_fusion = (f32[2,1280]{1,0:T(2,128)S(1)}, f32[2,2560]{1,0:T(2,128)S(1)}, f32[2,2560]{1,0:T(2,128)S(1)}) fusion(f32[2,2560,1280]{1,2,0:T(8,128)} %get-tuple-element.25, f32[2,1280]{1,0:T(2,128)S(1)} %broadcast_maximum_fusion, pred[2560,1280]{0,1:T(8,128)(4,1)} %broadcast_compare_fusion, f32[2,2560]{1,0:T(2,128)S(1)} %get-tuple-element.6), kind=kLoop, calls=%fused_computation | loop fusion | flops 39308800 | bytes 29573120 | tf_op jit(solution)/shard_map/reduce_sum | solution.py:99
  338.3 10.5 %all-gather.6 = f32[4,6,2560]{2,1,0:T(8,128)S(1)} all-gather(f32[1,6,2560]{2,1,0:T(8,128)S(1)} %maximum_bitcast_fusion), channel_id=2, replica_groups=mesh['wide_0'=4,'wide_1'=4,'wide_2'=2,'narrow_0'=2,'narrow_1'=2] {'wide_0'}, dimensions={0}, use_global_device_ids=true | all-gather | bytes 307200 | tf_op jit(solution)/shard_map/all_gather | solution.py:36
  348.8 0.1 fusion.47
  349.0 10.2 %all-gather.7 = f32[4,6,2560]{2,1,0:T(8,128)S(1)} all-gather(f32[1,6,2560]{2,1,0:T(8,128)S(1)} %maximum_bitcast_fusion.1), channel_id=3, replica_groups=mesh['wide_0'=4,'wide_1'=4,'wide_2'=2,'narrow_0'=2,'narrow_1'=2] {'wide_1'}, dimensions={0}, use_global_device_ids=true | all-gather | bytes 307200 | tf_op jit(solution)/shard_map/all_gather | solution.py:36
  359.4 5.5 %all-gather.8 = f32[2,6,2560]{2,1,0:T(8,128)S(1)} all-gather(f32[1,6,2560]{2,1,0:T(8,128)S(1)} %maximum_bitcast_fusion.2), channel_id=4, replica_groups=mesh['wide_0'=4,'wide_1'=4,'wide_2'=2,'narrow_0'=2,'narrow_1'=2] {'wide_2'}, dimensions={0}, use_global_device_ids=true | all-gather | bytes 184320 | tf_op jit(solution)/shard_map/all_gather | solution.py:36
  365.0 4.8 %all-gather.9 = f32[2,6,2560]{2,1,0:T(8,128)S(1)} all-gather(f32[1,6,2560]{2,1,0:T(8,128)S(1)} %maximum_bitcast_fusion.3), channel_id=5, replica_groups=mesh['wide_0'=4,'wide_1'=4,'wide_2'=2,'narrow_0'=2,'narrow_1'=2] {'narro..., dimensions={0}, use_global_device_ids=true | all-gather | bytes 184320 | tf_op jit(solution)/shard_map/all_gather | solution.py:36
  369.8 0.6 log_add_fusion
  370.5 7.2 %all-gather.10 = f32[2,6,2560]{2,1,0:T(8,128)S(1)} all-gather(f32[1,6,2560]{2,1,0:T(8,128)S(1)} %maximum_bitcast_fusion.4), channel_id=6, replica_groups=mesh['wide_0'=4,'wide_1'=4,'wide_2'=2,'narrow_0'=2,'narrow_1'=2] {'narro..., dimensions={0}, use_global_device_ids=true | all-gather | bytes 184320 | tf_op jit(solution)/shard_map/all_gather | solution.py:36
  377.8 0.6 fusion.64
  (47 shorter events, 0.8 us)
Async XLA Ops:
  7.2 218.8 %copy-start = (bf16[1280,1024]{1,0:T(8,128)(2,1)S(1)}, bf16[1280,1024]{1,0:T(8,128)(2,1)}, u32[]{:S(2)}) copy-start(bf16[1280,1024]{1,0:T(8,128)(2,1)} %param.8) | copy-start | bytes 7864324
  7.2 112.6 %copy-start.4 = (u32[128]{0:T(128)S(1)}, u32[128]{0:T(128)}, u32[]{:S(2)}) copy-start(u32[128]{0:T(128)} %constant.68) | copy-start | bytes 1540
  7.2 209.1 %all-gather.16.cloned.1.call-start = ((), (), s32[]{:S(2)}) async-start(), calls=%async_computation.1 | async-start | bytes 1622016 | tf_op jit(solution)/shard_map/all_gather | solution.py:25
  110.2 8.1 %collective-permute-start.5 = (bf16[4,1024]{1,0:T(4,128)(2,1)S(1)}, bf16[4,1024]{1,0:T(4,128)(2,1)S(1)}, u32[]{:S(2)}, u32[]{:S(2)}) collective-permute-start(bf16[4,1024]{1,0:T(4,128)(2,1)S(1)} %slice.293), channel_id=1, source_target_pairs={{0,24},{4,28},{8,32},{12,36},{16,40},{20,44},{24,48},{28,52},{32,5... | collective-permute-start | bytes 24584
  111.5 9.5 %collective-permute-start = (bf16[24,1024]{1,0:T(8,128)(2,1)S(1)}, bf16[24,1024]{1,0:T(8,128)(2,1)S(1)}, u32[]{:S(2)}, u32[]{:S(2)}) collective-permute-start(bf16[24,1024]{1,0:T(8,128)(2,1)S(1)} %fusion), channel_id=1, source_target_pairs={{0,4},{4,8},{8,12},{12,16},{16,20},{20,24},{24,28},{28,32},{32,36}... | collective-permute-start | bytes 147464
  112.8 8.2 %collective-permute-start.1 = (bf16[24,1024]{1,0:T(8,128)(2,1)S(1)}, bf16[24,1024]{1,0:T(8,128)(2,1)S(1)}, u32[]{:S(2)}, u32[]{:S(2)}) collective-permute-start(bf16[24,1024]{1,0:T(8,128)(2,1)S(1)} %fusion), channel_id=1, source_target_pairs={{0,8},{4,12},{8,16},{12,20},{16,24},{20,28},{24,32},{28,36},{32,40... | collective-permute-start | bytes 147464
  114.1 6.9 %collective-permute-start.2 = (bf16[24,1024]{1,0:T(8,128)(2,1)S(1)}, bf16[24,1024]{1,0:T(8,128)(2,1)S(1)}, u32[]{:S(2)}, u32[]{:S(2)}) collective-permute-start(bf16[24,1024]{1,0:T(8,128)(2,1)S(1)} %fusion), channel_id=1, source_target_pairs={{0,12},{4,16},{8,20},{12,24},{16,28},{20,32},{24,36},{28,40},{32,4... | collective-permute-start | bytes 147464
  115.4 5.6 %collective-permute-start.3 = (bf16[24,1024]{1,0:T(8,128)(2,1)S(1)}, bf16[24,1024]{1,0:T(8,128)(2,1)S(1)}, u32[]{:S(2)}, u32[]{:S(2)}) collective-permute-start(bf16[24,1024]{1,0:T(8,128)(2,1)S(1)} %fusion), channel_id=1, source_target_pairs={{0,16},{4,20},{8,24},{12,28},{16,32},{20,36},{24,40},{28,44},{32,4... | collective-permute-start | bytes 147464
  118.4 2.7 collective-permute-start.4
  122.7 180.5 %all-gather.14.cloned.1.call-start = ((), (), s32[]{:S(2)}) async-start(), calls=%async_computation | async-start | bytes 9830400 | tf_op jit(solution)/shard_map/all_gather | solution.py:86
  219.6 3.2 copy-start.2
  219.6 3.3 copy-start.5
  226.0 4.0 %copy-start.6 = (bf16[2,1024,768]{2,1,0:T(8,128)(2,1)S(1)}, bf16[2,1024,768]{2,1,0:T(8,128)(2,1)}, u32[]{:S(2)}) copy-start(bf16[2,1024,768]{2,1,0:T(8,128)(2,1)} %param.10) | copy-start | bytes 9437188
  232.4 2.0 copy-start.3
  234.4 68.8 %copy-start.7 = (f32[2]{0:T(128)S(1)}, f32[2]{0:T(128)}, u32[]{:S(2)}) copy-start(f32[2]{0:T(128)} %param.11) | copy-start | bytes 28
  322.9 55.5 %copy-start.1 = (bf16[1280,1024]{1,0:T(8,128)(2,1)S(1)}, bf16[1280,1024]{1,0:T(8,128)(2,1)}, u32[]{:S(2)}) copy-start(bf16[1280,1024]{1,0:T(8,128)(2,1)} %param.8) | copy-start | bytes 7864324
Sparse Core Ops, SparseCore 0:
  122.9 93.4 all-gather.15
  226.1 77.1 all-gather.13
where the time goes:
time: 386 us; the launch traced here: 385 us
  waiting for transfers between devices  159 us (41%)
  blocking collectives  138 us (36%)
  matrix products  30.5 us (8%)
  other arithmetic  27.1 us (7%)
  between operations  15.9 us (4%)
  starting transfers between devices  9.55 us (2%)
  local copies, waits for them, and re-layouts  5.57 us (1%)
    unnamed x1, blocking collectives  99.7 us
    all_gather x1, waiting for transfers between devices, from_root(): lax.all_gather(own, axis, axis=0, tiled=True)[:len(lines)]  93.5 us
    all_gather x1, waiting for transfers between devices, per_device(): piece = lax.all_gather(band_emb, NARROW, axis=1, tiled=True)  65.2 us
    all_gather x5, blocking collectives, collected_together(): both, at, found = (lax.all_gather(jnp.concatenate(lines), axis), 0, {})  38.1 us
    dot_general x1, matrix products, per_device(): jnp.einsum('hid,hjd->hij', piece, text_emb, preferred_element_type=jnp.fl...  19.6 us
    reduce_sum x1, other arithmetic, per_device(): col_sum = jnp.sum(jnp.exp(logits - new_max[:, None, :]), axis=1)  15.4 us
    dot_general x4, matrix products, embed(): full = jnp.dot(tower, weight, preferred_element_type=jnp.float32)  10.9 us
    unnamed x6, starting transfers between devices  9.47 us
  transfers between devices with their start and end apart: 8, of which 2 were waited for; matrix products, arithmetic and copies ran while one was open for 3% of the time, Pallas kernels for 0%

commit v1 on v0

--- a/solution.py
+++ b/solution.py
@@ -3,6 +3,7 @@
 from jax import lax
 from jax.sharding import Mesh
 from jax.sharding import PartitionSpec as P
+from jax.lax import all_to_all, axis_size
 
 WIDE = ("wide_0", "wide_1", "wide_2")
 NARROW = ("narrow_0", "narrow_1")
@@ -22,7 +23,14 @@
     )
     padded = filled_up(lines, lax.axis_size(axis))
     own = lax.psum_scatter(padded, axis, scatter_dimension=0, tiled=True)
-    return lax.all_gather(own, axis, axis=0, tiled=True)[: len(lines)].reshape(value.shape)
+
+    def deliver_the_turns(packet, ndim_at):
+        val = jnp.concatenate(
+            all_to_all(jnp.stack(axis_size(axis) * [packet], 0), axis, 0, 0), ndim_at
+        )
+        return val
+
+    return deliver_the_turns(own, ndim_at=0)[: len(lines)].reshape(value.shape)
 
 
 def collected_together(value, axis):

time: 386 us -> 341 us (0.88)
  waiting for transfers between devices: 159 us -> 80 us
  blocking collectives: 138 us -> 173 us
    all_gather x1 -> x0, waiting for transfers between devices: 93.5 us -> none  [from_root(): lax.all_gather(own, axis, axis=0, tiled=True)[:len(lines)]]
    all_to_all x0 -> x1, blocking collectives: none -> 34.8 us  [deliver_the_turns(): all_to_all(jnp.stack(axis_size(axis) * [packet], 0), axis, 0, 0)]
    all_gather x1, waiting for transfers between devices: 65.2 us -> 79.9 us  [per_device(): piece = lax.all_gather(band_emb, NARROW, axis=1, tiled=True)]
    unnamed x21 -> x20, local copies, waits for them, and re-layouts: 5.55 us -> 1.66 us
  transfers between devices with their start and end apart: 8 -> 7, of which waited for: 2 -> 1; matrix products, arithmetic and copies ran while one was open for 3% -> 4% of each run, Pallas kernels for 0% -> 0%
where the time goes in v1:
time: 341 us
  blocking collectives  173 us (51%)
  waiting for transfers between devices  80 us (23%)
  matrix products  30.5 us (9%)
  other arithmetic  27.1 us (8%)
  between operations  15.9 us (5%)
  starting transfers between devices  9.51 us (3%)
  local copies, waits for them, and re-layouts  5.13 us (2%)
    unnamed x1, blocking collectives  99.7 us
    all_gather x1, waiting for transfers between devices, per_device(): piece = lax.all_gather(band_emb, NARROW, axis=1, tiled=True)  79.9 us
    all_gather x5, blocking collectives, collected_together(): both, at, found = (lax.all_gather(jnp.concatenate(lines), axis), 0, {})  38.1 us
    all_to_all x1, blocking collectives, deliver_the_turns(): all_to_all(jnp.stack(axis_size(axis) * [packet], 0), axis, 0, 0)  34.8 us
    dot_general x1, matrix products, per_device(): jnp.einsum('hid,hjd->hij', piece, text_emb, preferred_element_type=jnp.fl...  19.6 us
    reduce_sum x1, other arithmetic, per_device(): col_sum = jnp.sum(jnp.exp(logits - new_max[:, None, :]), axis=1)  15.3 us
    dot_general x4, matrix products, embed(): full = jnp.dot(tower, weight, preferred_element_type=jnp.float32)  10.9 us
    unnamed x6, starting transfers between devices  9.47 us
  transfers between devices with their start and end apart: 7, of which 1 were waited for; matrix products, arithmetic and copies ran while one was open for 4% of the time, Pallas kernels for 0%

profile of v1, /device:TPU:1, one launch (start us, length us, event | category | flops | bytes accessed | tf_op | source)
XLA Modules:
  0.0 340.6 jit_solution(4437588928815566906)
XLA Ops:
  8.1 2.5 select_bitcast_fusion
  10.5 99.7 %fusion = bf16[24,1024]{1,0:T(8,128)(2,1)S(1)} fusion(bf16[640,1024]{1,0:T(8,128)(2,1)} %select_bitcast_fusion), kind=kCustom, calls=%all-reduce-scatter | all-reduce-scatter fusion | flops 786433 | bytes 1360384
  110.2 1.3 collective-permute-start.5
  111.5 1.3 collective-permute-start
  112.8 1.3 collective-permute-start.1
  114.1 1.3 collective-permute-start.2
  115.4 2.9 collective-permute-start.3
  118.3 1.4 collective-permute-start.4
  119.8 0.6 dynamic-slice.5
  121.1 1.0 concatenate.20
  122.1 0.2 stack.14
  122.3 34.8 %all_to_all.5 = bf16[32,20,1024]{2,1,0:T(8,128)(2,1)} all-to-all(bf16[32,20,1024]{2,1,0:T(8,128)(2,1)S(1)} %stack.14), channel_id=1, replica_groups=mesh['wide_0'=4,'wide_1'=4,'wide_2'=2,'narrow_0'=2,'narrow_1'=2] {'wide_..., dimensions={0} | all-to-all | bytes 2621440 | tf_op jit(solution)/shard_map/all_to_all | solution.py:29
  157.1 3.3 reshape.114
  160.4 3.2 multiply_reduce_fusion.2
  163.6 1.3 multiply_reduce_fusion.3
  164.9 0.3 fusion.18
  165.2 1.5 pad_maximum_fusion
  166.7 4.0 %multiply_reduce_fusion = (f32[1280]{0:T(1024)S(1)}, f32[1280,768]{0,1:T(8,128)S(1)}) fusion(bf16[1280,1024]{1,0:T(8,128)(2,1)S(1)} %copy-done, bf16[2,1024,768]{2,1,0:T(8,128)(2,1)} %param.10), kind=kOutput, calls=%fused_computation.9 | convolution fusion | flops 2015230720 | bytes 8131584 | tf_op jit(solution)/shard_map/dot_general | solution.py:63
  170.7 2.4 multiply_reduce_fusion.1
  173.2 2.0 fusion.4
  175.2 3.6 %broadcast_compare_fusion = pred[2560,1280]{0,1:T(8,128)(4,1)} fusion(s32[2560]{0:T(1024)S(1)} %iota_add_fusion, s32[1280]{0:T(1024)S(1)} %copy-done.3), kind=kLoop, calls=%fused_computation.4 | loop fusion | flops 3276800 | bytes 3292160 | tf_op jit(solution)/shard_map/eq | solution.py:101
  178.8 79.9 %all-gather.12.cloned.1.call-done = bf16[2,2560,768]{2,1,0:T(8,128)(2,1)} async-done(((bf16[2,640,768]{2,1,0:T(8,128)(2,1)}), bf16[2,2560,768]{2,1,0:T(8,128)(2,1)}) %all-gather.12.cloned.1.call-update) | async-done | bytes 7864336 | tf_op jit(solution)/shard_map/all_gather | solution.py:94
  258.7 19.6 %fusion.66 = (f32[2,1280]{1,0:T(2,128)S(1)}, f32[2,2560]{1,0:T(2,128)S(1)}, f32[2,2560,1280]{1,2,0:T(8,128)}) fusion(bf16[2,2560,768]{2,1,0:T(8,128)(2,1)} %all-gather.12.cloned.1.call-done, bf16[1,1280,768]{1,2,0:T(8,128)(2,1)} %get-tuple-element.29, bf16[1,1280,768]{1,2,0:T(8,128)(2,1)S(1)} %get-tuple-element.28, f32[2]{0:T(128)S(1)} %copy-done.7), kind=kOutput, calls=%fused_computation.132 | convolution fusion | flops 10087949312 | bytes 38041608 | tf_op jit(solution)/shard_map/hid,hjd->hij/dot_general | solution.py:97
  278.4 15.3 %exponential_reduce_fusion = (f32[2,1280]{1,0:T(2,128)S(1)}, f32[2,2560]{1,0:T(2,128)S(1)}, f32[2,2560]{1,0:T(2,128)S(1)}) fusion(f32[2,2560,1280]{1,2,0:T(8,128)} %get-tuple-element.25, f32[2,1280]{1,0:T(2,128)S(1)} %broadcast_maximum_fusion, pred[2560,1280]{0,1:T(8,128)(4,1)} %broadcast_compare_fusion, f32[2,2560]{1,0:T(2,128)S(1)} %get-tuple-element.6), kind=kLoop, calls=%fused_computation | loop fusion | flops 39308800 | bytes 29573120 | tf_op jit(solution)/shard_map/reduce_sum | solution.py:107
  293.7 10.5 %all-gather.5 = f32[4,6,2560]{2,1,0:T(8,128)S(1)} all-gather(f32[1,6,2560]{2,1,0:T(8,128)S(1)} %maximum_bitcast_fusion), channel_id=2, replica_groups=mesh['wide_0'=4,'wide_1'=4,'wide_2'=2,'narrow_0'=2,'narrow_1'=2] {'wide_0'}, dimensions={0}, use_global_device_ids=true | all-gather | bytes 307200 | tf_op jit(solution)/shard_map/all_gather | solution.py:44
  304.2 0.1 fusion.47
  304.4 10.2 %all-gather.6 = f32[4,6,2560]{2,1,0:T(8,128)S(1)} all-gather(f32[1,6,2560]{2,1,0:T(8,128)S(1)} %maximum_bitcast_fusion.1), channel_id=3, replica_groups=mesh['wide_0'=4,'wide_1'=4,'wide_2'=2,'narrow_0'=2,'narrow_1'=2] {'wide_1'}, dimensions={0}, use_global_device_ids=true | all-gather | bytes 307200 | tf_op jit(solution)/shard_map/all_gather | solution.py:44
  314.8 5.5 %all-gather.7 = f32[2,6,2560]{2,1,0:T(8,128)S(1)} all-gather(f32[1,6,2560]{2,1,0:T(8,128)S(1)} %maximum_bitcast_fusion.2), channel_id=4, replica_groups=mesh['wide_0'=4,'wide_1'=4,'wide_2'=2,'narrow_0'=2,'narrow_1'=2] {'wide_2'}, dimensions={0}, use_global_device_ids=true | all-gather | bytes 184320 | tf_op jit(solution)/shard_map/all_gather | solution.py:44
  320.4 4.8 %all-gather.8 = f32[2,6,2560]{2,1,0:T(8,128)S(1)} all-gather(f32[1,6,2560]{2,1,0:T(8,128)S(1)} %maximum_bitcast_fusion.3), channel_id=5, replica_groups=mesh['wide_0'=4,'wide_1'=4,'wide_2'=2,'narrow_0'=2,'narrow_1'=2] {'narro..., dimensions={0}, use_global_device_ids=true | all-gather | bytes 184320 | tf_op jit(solution)/shard_map/all_gather | solution.py:44
  325.2 0.6 log_add_fusion
  325.9 7.2 %all-gather.9 = f32[2,6,2560]{2,1,0:T(8,128)S(1)} all-gather(f32[1,6,2560]{2,1,0:T(8,128)S(1)} %maximum_bitcast_fusion.4), channel_id=6, replica_groups=mesh['wide_0'=4,'wide_1'=4,'wide_2'=2,'narrow_0'=2,'narrow_1'=2] {'narro..., dimensions={0}, use_global_device_ids=true | all-gather | bytes 184320 | tf_op jit(solution)/shard_map/all_gather | solution.py:44
  333.2 0.6 fusion.64
  (46 shorter events, 0.8 us)
Async XLA Ops:
  7.2 159.6 %copy-start = (bf16[1280,1024]{1,0:T(8,128)(2,1)S(1)}, bf16[1280,1024]{1,0:T(8,128)(2,1)}, u32[]{:S(2)}) copy-start(bf16[1280,1024]{1,0:T(8,128)(2,1)} %param.8) | copy-start | bytes 7864324
  7.2 112.6 %copy-start.4 = (u32[128]{0:T(128)S(1)}, u32[128]{0:T(128)}, u32[]{:S(2)}) copy-start(u32[128]{0:T(128)} %constant.68) | copy-start | bytes 1540
  7.2 251.5 %all-gather.12.cloned.1.call-start = ((), (), s32[]{:S(2)}) async-start(), calls=%async_computation.1 | async-start | bytes 9830400 | tf_op jit(solution)/shard_map/all_gather | solution.py:94
  110.2 8.1 %collective-permute-start.5 = (bf16[4,1024]{1,0:T(4,128)(2,1)S(1)}, bf16[4,1024]{1,0:T(4,128)(2,1)S(1)}, u32[]{:S(2)}, u32[]{:S(2)}) collective-permute-start(bf16[4,1024]{1,0:T(4,128)(2,1)S(1)} %slice.293), channel_id=1, source_target_pairs={{0,24},{4,28},{8,32},{12,36},{16,40},{20,44},{24,48},{28,52},{32,5... | collective-permute-start | bytes 24584
  111.5 9.5 %collective-permute-start = (bf16[24,1024]{1,0:T(8,128)(2,1)S(1)}, bf16[24,1024]{1,0:T(8,128)(2,1)S(1)}, u32[]{:S(2)}, u32[]{:S(2)}) collective-permute-start(bf16[24,1024]{1,0:T(8,128)(2,1)S(1)} %fusion), channel_id=1, source_target_pairs={{0,4},{4,8},{8,12},{12,16},{16,20},{20,24},{24,28},{28,32},{32,36}... | collective-permute-start | bytes 147464
  112.8 8.2 %collective-permute-start.1 = (bf16[24,1024]{1,0:T(8,128)(2,1)S(1)}, bf16[24,1024]{1,0:T(8,128)(2,1)S(1)}, u32[]{:S(2)}, u32[]{:S(2)}) collective-permute-start(bf16[24,1024]{1,0:T(8,128)(2,1)S(1)} %fusion), channel_id=1, source_target_pairs={{0,8},{4,12},{8,16},{12,20},{16,24},{20,28},{24,32},{28,36},{32,40... | collective-permute-start | bytes 147464
  114.1 6.9 %collective-permute-start.2 = (bf16[24,1024]{1,0:T(8,128)(2,1)S(1)}, bf16[24,1024]{1,0:T(8,128)(2,1)S(1)}, u32[]{:S(2)}, u32[]{:S(2)}) collective-permute-start(bf16[24,1024]{1,0:T(8,128)(2,1)S(1)} %fusion), channel_id=1, source_target_pairs={{0,12},{4,16},{8,20},{12,24},{16,28},{20,32},{24,36},{28,40},{32,4... | collective-permute-start | bytes 147464
  115.4 5.6 %collective-permute-start.3 = (bf16[24,1024]{1,0:T(8,128)(2,1)S(1)}, bf16[24,1024]{1,0:T(8,128)(2,1)S(1)}, u32[]{:S(2)}, u32[]{:S(2)}) collective-permute-start(bf16[24,1024]{1,0:T(8,128)(2,1)S(1)} %fusion), channel_id=1, source_target_pairs={{0,16},{4,20},{8,24},{12,28},{16,32},{20,36},{24,40},{28,44},{32,4... | collective-permute-start | bytes 147464
  118.3 2.7 collective-permute-start.4
  160.3 3.2 copy-start.2
  160.4 3.3 copy-start.5
  166.7 4.0 %copy-start.6 = (bf16[2,1024,768]{2,1,0:T(8,128)(2,1)S(1)}, bf16[2,1024,768]{2,1,0:T(8,128)(2,1)}, u32[]{:S(2)}) copy-start(bf16[2,1024,768]{2,1,0:T(8,128)(2,1)} %param.10) | copy-start | bytes 9437188
  173.2 2.0 copy-start.3
  175.2 83.5 %copy-start.7 = (f32[2]{0:T(128)S(1)}, f32[2]{0:T(128)}, u32[]{:S(2)}) copy-start(f32[2]{0:T(128)} %param.11) | copy-start | bytes 28
  278.3 55.5 %copy-start.1 = (bf16[1280,1024]{1,0:T(8,128)(2,1)S(1)}, bf16[1280,1024]{1,0:T(8,128)(2,1)}, u32[]{:S(2)}) copy-start(bf16[1280,1024]{1,0:T(8,128)(2,1)} %param.8) | copy-start | bytes 7864324
Sparse Core Ops, SparseCore 0:
  166.8 91.8 all-gather.11
